TPU v7x, 32 devices: a whole 2x2x4 slice. The times are simulated.
32 devices in a mesh: rep: 1, r: 4 (over z), s: 8 (over x, y, core).
Axes of the slice: x: 2, y: 2, z: 4, core: 2. Of those that a mesh axis runs over, the one named last changes fastest.
Arguments:
- x: bfloat16 [32, 4096, 512], P(('rep', 'r', 's'))
- dy: bfloat16 [32, 4096, 512], P(('rep', 'r', 's'))
- w_gate: bfloat16 [2, 512, 1280], P(None, 's')
- w_up: bfloat16 [2, 512, 1280], P(None, 's')
- w_down: bfloat16 [2, 1280, 512], P(None, 's')
Outputs:
- output 1: bfloat16 [32, 4096, 512], P(('rep', 'r', 's'))
- output 2: bfloat16 [2, 512, 1280], P('rep', 's')
- output 3: bfloat16 [2, 512, 1280], P('rep', 's')
- output 4: bfloat16 [2, 1280, 512], P('rep', 's')
All inputs are finite; a program needn't handle non-finite values.
Results may differ from a plain program's by a relative error of at most 0.018.
Values are sent between devices in bfloat16 or wider.
A program may use at most 2 GiB of HBM per device.

v0:
```python
import jax
import jax.numpy as jnp
from jax import lax
from jax.sharding import PartitionSpec as P

NAMES = ("w_gate", "w_up", "w_down")


def matmul(a, w):
    return jnp.dot(a, w, preferred_element_type=jnp.float32).astype(jnp.bfloat16)


def normed(h):
    wide = h.astype(jnp.float32)
    scale = lax.rsqrt(jnp.mean(wide**2, -1, keepdims=True) + 1e-6)
    return (wide * scale).astype(jnp.bfloat16)


def layer(h, w):
    a = normed(h)
    gate = jnp.dot(a, w["w_gate"], preferred_element_type=jnp.float32)
    up = jnp.dot(a, w["w_up"], preferred_element_type=jnp.float32)
    return h + matmul((jax.nn.silu(gate) * up).astype(jnp.bfloat16), w["w_down"])


def solution(mesh):
    def fetched(weights, number):
        return {name: lax.all_gather(w[number], "s", axis=0, tiled=True) for name, w in zip(NAMES, weights, strict=True)}

    def summed(term):
        return lax.psum(lax.psum_scatter(term, "s", scatter_dimension=0, tiled=True), "r")

    def step(x, dy, *weights):
        layers = weights[0].shape[0]
        h, inputs = x[0], []
        for number in range(layers):
            inputs.append(h)
            h = layer(h, fetched(weights, number))
        by_h, mine = dy[0], [None] * layers
        for number in reversed(range(layers)):
            _, back = jax.vjp(lambda w, h: layer(h, w), fetched(weights, number), inputs[number])
            by_w, by_h = back(by_h)
            mine[number] = [summed(by_w[name]) for name in NAMES]
        return (by_h[None], *(jnp.stack([mine[number][i] for number in range(layers)]) for i in range(3)))

    states, cut = P(("rep", "r", "s"), None, None), P(None, "s", None)
    return jax.shard_map(
        step,
        mesh=mesh,
        in_specs=(states, states) + (cut,) * 3,
        out_specs=(states,) + (P("rep", "s", None),) * 3,
        check_vma=False,
    )
```

profile of v0, /device:TPU:0, one launch (start us, length us, event | category | flops | bytes accessed | tf_op | source)
XLA Modules:
  0.0 518.5 jit_solution(9796710515522687975)
XLA Ops:
  7.2 1.7 fusion.66
  9.0 0.0 all-gather.15.cloned.1.call-start
  9.0 1.7 fusion.67
  10.8 1.8 fusion.68
  12.7 0.5 all-gather.21.cloned.1.call-update
  13.2 0.5 all-gather.23.cloned.1.call-update
  13.8 0.5 all-gather.19.cloned.1.call-update
  14.4 6.3 %copy.10 = bf16[1,4096,512]{1,2,0:T(8,128)(2,1)} copy(bf16[1,4096,512]{2,1,0:T(8,128)(2,1)} %param.5) | data formatting | bytes 8388608 | tf_op args[0]
  20.7 3.1 fusion.15
  23.8 0.6 copy-done.3
  24.4 6.4 %copy.9 = bf16[1,4096,512]{1,2,0:T(8,128)(2,1)} copy(bf16[1,4096,512]{2,1,0:T(8,128)(2,1)} %param.6) | data formatting | bytes 8388608 | tf_op args[1]
  30.9 6.6 %all-gather.13.cloned.1.call-done = bf16[1,512,1280]{2,1,0:T(8,128)(2,1)} async-done(((bf16[1,64,1280]{2,1,0:T(8,128)(2,1)}), bf16[1,512,1280]{2,1,0:T(8,128)(2,1)}) %all-gather.13.cloned.1.call-update) | async-done | bytes 1310736 | tf_op jit(solution)/shard_map/all_gather | solution.py:28
  37.4 11.9 %fusion.46 = f32[4096,1280]{1,0:T(8,128)} fusion(bf16[1,4096,512]{1,2,0:T(8,128)(2,1)} %copy.10, f32[4096]{0:T(1024)S(1)} %fusion.59, bf16[1,512,1280]{2,1,0:T(8,128)(2,1)} %all-gather.13.cloned.1.call-done), kind=kOutput, calls=%fused_computation.65 | convolution fusion | flops 5375000576 | bytes 26492928 | tf_op jit(solution)/shard_map/dot_general | solution.py:21
  49.3 14.2 %all-gather.15.cloned.1.call-done = bf16[1,512,1280]{2,1,0:T(8,128)(2,1)} async-done(((bf16[1,64,1280]{2,1,0:T(8,128)(2,1)}), bf16[1,512,1280]{2,1,0:T(8,128)(2,1)}) %all-gather.15.cloned.1.call-update) | async-done | bytes 1310736 | tf_op jit(solution)/shard_map/all_gather | solution.py:28
  63.5 19.2 %multiply_convert_fusion.1 = (bf16[4096,1280]{1,0:T(8,128)(2,1)}, f32[4096,1280]{1,0:T(8,128)}) fusion(f32[4096,1280]{1,0:T(8,128)} %fusion.46, bf16[1,512,1280]{2,1,0:T(8,128)(2,1)} %all-gather.15.cloned.1.call-done, bf16[1,4096,512]{1,2,0:T(8,128)(2,1)} %copy.10, f32[4096]{0:T(1024)S(1)} %fusion.59), kind=kOutput, calls=%fused_computation.13 | convolution fusion | flops 5406457856 | bytes 57950208 | tf_op jit(solution)/shard_map/dot_general | solution.py:22
  82.7 7.0 %all-gather.17.cloned.1.call-done = bf16[1,1280,512]{2,1,0:T(8,128)(2,1)} async-done(((bf16[1,160,512]{2,1,0:T(8,128)(2,1)}), bf16[1,1280,512]{2,1,0:T(8,128)(2,1)}) %all-gather.17.cloned.1.call-update) | async-done | bytes 1310736 | tf_op jit(solution)/shard_map/all_gather | solution.py:28
  89.7 11.2 %fusion.18 = (f32[4096]{0:T(1024)S(1)}, bf16[4096,512]{0,1:T(8,128)(2,1)}) fusion(bf16[4096,1280]{1,0:T(8,128)(2,1)} %get-tuple-element.20, bf16[1,1280,512]{2,1,0:T(8,128)(2,1)} %all-gather.17.cloned.1.call-done, bf16[1,4096,512]{1,2,0:T(8,128)(2,1)} %copy.10), kind=kOutput, calls=%fused_computation.40 | convolution fusion | flops 5379190784 | bytes 20201472 | tf_op jit(solution)/shard_map/dot_general | solution.py:10
  100.9 0.6 copy-done.5
  101.5 14.1 %all-gather.21.cloned.1.call-done = bf16[1,1280,512]{2,1,0:T(8,128)(2,1)} async-done(((bf16[1,160,512]{2,1,0:T(8,128)(2,1)}), bf16[1,1280,512]{2,1,0:T(8,128)(2,1)}) %all-gather.21.cloned.1.call-update) | async-done | bytes 1310736 | tf_op jit(solution)/shard_map/all_gather | solution.py:28
  115.7 10.3 %convolution_convert_fusion.1 = bf16[4096,1280]{1,0:T(8,128)(2,1)} fusion(bf16[1,4096,512]{2,1,0:T(8,128)(2,1)} %param.6, bf16[1,1280,512]{2,1,0:T(8,128)(2,1)} %all-gather.21.cloned.1.call-done), kind=kOutput, calls=%fused_computation.17 | convolution fusion | flops 5373952000 | bytes 15990784 | tf_op jit(solution)/shard_map/transpose(jvp())/dot_general | solution.py:10
  125.9 16.3 %all-gather.23.cloned.1.call-done = bf16[1,512,1280]{2,1,0:T(8,128)(2,1)} async-done(((bf16[1,64,1280]{2,1,0:T(8,128)(2,1)}), bf16[1,512,1280]{2,1,0:T(8,128)(2,1)}) %all-gather.23.cloned.1.call-update) | async-done | bytes 1310736 | tf_op jit(solution)/shard_map/all_gather | solution.py:28
  142.2 12.0 %fusion.38 = f32[4096,1280]{1,0:T(8,128)} fusion(bf16[4096,512]{0,1:T(8,128)(2,1)} %get-tuple-element.23, f32[4096]{0:T(1024)S(1)} %fusion.60, bf16[1,512,1280]{2,1,0:T(8,128)(2,1)} %all-gather.23.cloned.1.call-done), kind=kOutput, calls=%fused_computation.62 | convolution fusion | flops 5375000576 | bytes 26492928 | tf_op jit(solution)/shard_map/jvp()/dot_general | solution.py:22
  154.2 14.6 %all-gather.19.cloned.1.call-done = bf16[1,512,1280]{2,1,0:T(8,128)(2,1)} async-done(((bf16[1,64,1280]{2,1,0:T(8,128)(2,1)}), bf16[1,512,1280]{2,1,0:T(8,128)(2,1)}) %all-gather.19.cloned.1.call-update) | async-done | bytes 1310736 | tf_op jit(solution)/shard_map/all_gather | solution.py:28
  168.7 28.8 %fusion.1 = (bf16[4096,1280]{1,0:T(8,128)(2,1)}, f32[4096,1280]{1,0:T(8,128)}) fusion(f32[4096,1280]{1,0:T(8,128)} %fusion.38, bf16[4096,1280]{1,0:T(8,128)(2,1)} %convolution_convert_fusion.1, bf16[1,512,1280]{2,1,0:T(8,128)(2,1)} %all-gather.19.cloned.1.call-done, bf16[4096,512]{0,1:T(8,128)(2,1)} %get-tuple-element.23, f32[4096]{0:T(1024)S(1)} %fusion.60), kind=kOutput, calls=%fused_computation.7 | convolution fusion | flops 5437915136 | bytes 68435968 | tf_op jit(solution)/shard_map/jvp()/dot_general | solution.py:21
  197.5 18.6 %fusion.31 = bf16[1280,512]{1,0:T(8,128)(2,1)} fusion(bf16[1,4096,512]{2,1,0:T(8,128)(2,1)} %param.6, f32[4096,1280]{1,0:T(8,128)} %fusion.38, f32[4096,1280]{1,0:T(8,128)} %get-tuple-element.25), kind=kOutput, calls=%fused_computation.56 | convolution fusion | flops 5400821760 | bytes 47448064 | tf_op jit(solution)/shard_map/transpose(jvp())/dot_general | solution.py:10
  216.2 15.3 %fusion.22 = bf16[4096,512]{0,1:T(8,128)(2,1)} fusion(bf16[4096,1280]{1,0:T(8,128)(2,1)} %convolution_convert_fusion.1, bf16[1,512,1280]{2,1,0:T(8,128)(2,1)S(1)} %copy-done.12, f32[4096,1280]{1,0:T(8,128)} %get-tuple-element.25), kind=kOutput, calls=%fused_computation.45 | convolution fusion | flops 5402263552 | bytes 36962304 | tf_op jit(solution)/shard_map/transpose(jvp())/dot_general | solution.py:22
  231.5 12.7 %fusion.20 = (f32[4096]{0:T(1024)S(1)}, bf16[4096,512]{0,1:T(8,128)(2,1)}) fusion(bf16[4096,512]{0,1:T(8,128)(2,1)S(1)} %copy-done.2, bf16[4096,512]{0,1:T(8,128)(2,1)} %fusion.22, bf16[4096,1280]{1,0:T(8,128)(2,1)} %get-tuple-element.24, bf16[1,512,1280]{2,1,0:T(8,128)(2,1)S(1)} %copy-done.13), kind=kOutput, calls=%fused_computation.42 | convolution fusion | flops 5379190784 | bytes 24395776 | tf_op jit(solution)/shard_map/transpose(jvp())/dot_general | solution.py:21
  244.3 6.7 %convolution_convert_fusion.5 = bf16[512,1280]{1,0:T(8,128)(2,1)} fusion(bf16[4096,1280]{1,0:T(8,128)(2,1)S(1)} %copy-done.14, bf16[4096,512]{0,1:T(8,128)(2,1)S(1)} %copy-done.2, f32[4096]{0:T(1024)S(1)} %fusion.60), kind=kOutput, calls=%fused_computation.57 | convolution fusion | flops 5375000576 | bytes 16007168 | tf_op jit(solution)/shard_map/transpose(jvp())/dot_general | solution.py:21
  251.0 0.0 reduce-scatter.15.cloned.1.call-start
  251.0 6.2 %fusion.28 = bf16[4096,512]{0,1:T(8,128)(2,1)S(1)} fusion(bf16[4096,512]{0,1:T(8,128)(2,1)} %get-tuple-element.23, bf16[4096,512]{0,1:T(8,128)(2,1)} %get-tuple-element.27, bf16[1,4096,512]{1,2,0:T(8,128)(2,1)} %copy.9, f32[4096]{0:T(1024)S(1)} %multiply_multiply_fusion.1, f32[4096]{0:T(1024)S(1)} %fusion.60), kind=kLoop, calls=%fused_computation.53 | loop fusion | flops 14680064 | bytes 16809984 | tf_op jit(solution)/shard_map/transpose(jvp())/add_any | solution.py:14
  257.2 2.0 copy-done.1
  259.2 9.6 %convolution_convert_fusion.7 = bf16[1280,512]{1,0:T(8,128)(2,1)} fusion(bf16[4096,1280]{1,0:T(8,128)(2,1)} %get-tuple-element.20, bf16[4096,512]{0,1:T(8,128)(2,1)S(1)} %fusion.28), kind=kOutput, calls=%fused_computation.61 | convolution fusion | flops 5369364480 | bytes 15990784 | tf_op jit(solution)/shard_map/transpose(jvp())/dot_general | solution.py:10
  268.9 0.0 reduce-scatter.13.cloned.1.call-start
  268.9 16.3 %fusion.35 = bf16[512,1280]{1,0:T(8,128)(2,1)} fusion(bf16[4096,1280]{1,0:T(8,128)(2,1)} %convolution_convert_fusion.1, bf16[4096,512]{0,1:T(8,128)(2,1)} %get-tuple-element.23, f32[4096]{0:T(1024)S(1)} %fusion.60, f32[4096,1280]{1,0:T(8,128)} %get-tuple-element.25), kind=kOutput, calls=%fused_computation.60 | convolution fusion | flops 5407113216 | bytes 36978688 | tf_op jit(solution)/shard_map/transpose(jvp())/dot_general | solution.py:22
  285.3 0.0 reduce-scatter.7.cloned.1.call-start
  285.4 27.7 %fusion.3 = (bf16[4096,1280]{1,0:T(8,128)(2,1)}, bf16[4096,1280]{1,0:T(8,128)(2,1)}) fusion(f32[4096,1280]{1,0:T(8,128)} %fusion.46, f32[4096,1280]{1,0:T(8,128)} %get-tuple-element.21, bf16[4096,512]{0,1:T(8,128)(2,1)} %copy-done.1, bf16[1,1280,512]{2,1,0:T(8,128)(2,1)S(1)} %copy-done.11), kind=kOutput, calls=%fused_computation.9 | convolution fusion | flops 5436866560 | bytes 68419584 | tf_op jit(solution)/shard_map/transpose(jvp())/dot_general | solution.py:10
  313.1 11.2 %convolution_convert_fusion.6 = bf16[512,1280]{1,0:T(8,128)(2,1)} fusion(bf16[4096,1280]{1,0:T(8,128)(2,1)} %get-tuple-element.28, bf16[1,4096,512]{1,2,0:T(8,128)(2,1)} %copy.10, f32[4096]{0:T(1024)S(1)} %copy-done.8), kind=kOutput, calls=%fused_computation.58 | convolution fusion | flops 5375000576 | bytes 16007168 | tf_op jit(solution)/shard_map/transpose(jvp())/dot_general | solution.py:21
  324.4 16.4 %fusion.34 = bf16[512,1280]{1,0:T(8,128)(2,1)} fusion(bf16[4096,1280]{1,0:T(8,128)(2,1)} %get-tuple-element.29, bf16[1,4096,512]{1,2,0:T(8,128)(2,1)} %copy.10, f32[4096]{0:T(1024)S(1)} %copy-done.8, f32[4096,1280]{1,0:T(8,128)} %fusion.46), kind=kOutput, calls=%fused_computation.59 | convolution fusion | flops 5407113216 | bytes 36978688 | tf_op jit(solution)/shard_map/transpose(jvp())/dot_general | solution.py:22
  340.8 15.6 %fusion.21 = bf16[4096,512]{0,1:T(8,128)(2,1)} fusion(bf16[4096,1280]{1,0:T(8,128)(2,1)} %get-tuple-element.29, bf16[1,512,1280]{2,1,0:T(8,128)(2,1)S(1)} %copy-done.10, f32[4096,1280]{1,0:T(8,128)} %fusion.46), kind=kOutput, calls=%fused_computation.44 | convolution fusion | flops 5402263552 | bytes 36962304 | tf_op jit(solution)/shard_map/transpose(jvp())/dot_general | solution.py:22
  356.5 12.4 %fusion.17 = (f32[4096]{0:T(1024)S(1)}, bf16[4096,512]{0,1:T(8,128)(2,1)}) fusion(bf16[1,4096,512]{1,2,0:T(8,128)(2,1)S(1)} %copy-done, bf16[4096,512]{0,1:T(8,128)(2,1)} %fusion.21, bf16[4096,1280]{1,0:T(8,128)(2,1)} %get-tuple-element.28, bf16[1,512,1280]{2,1,0:T(8,128)(2,1)S(1)} %copy-done.9), kind=kOutput, calls=%fused_computation.39 | convolution fusion | flops 5379190784 | bytes 24395776 | tf_op jit(solution)/shard_map/transpose(jvp())/dot_general | solution.py:21
  368.9 5.2 %reduce-scatter.13.cloned.1.call-done = bf16[64,1280]{1,0:T(8,128)(2,1)} async-done(((bf16[512,1280]{1,0:T(8,128)(2,1)}), bf16[64,1280]{1,0:T(8,128)(2,1)}) %reduce-scatter.13.cloned.1.call-update) | async-done | bytes 163856 | tf_op jit(solution)/shard_map/reduce_scatter | solution.py:31
  374.2 40.3 %reduce-scatter.7.cloned.1.call-done = bf16[64,1280]{1,0:T(8,128)(2,1)} async-done(((bf16[512,1280]{1,0:T(8,128)(2,1)}), bf16[64,1280]{1,0:T(8,128)(2,1)}) %reduce-scatter.7.cloned.1.call-update) | async-done | bytes 163856 | tf_op jit(solution)/shard_map/reduce_scatter | solution.py:31
  414.5 40.2 %reduce-scatter.11.cloned.1.call-done = bf16[64,1280]{1,0:T(8,128)(2,1)} async-done(((bf16[512,1280]{1,0:T(8,128)(2,1)}), bf16[64,1280]{1,0:T(8,128)(2,1)}) %reduce-scatter.11.cloned.1.call-update) | async-done | bytes 163856 | tf_op jit(solution)/shard_map/reduce_scatter | solution.py:31
  454.7 7.6 %fusion.27 = bf16[1,4096,512]{1,2,0:T(8,128)(2,1)} fusion(bf16[4096,512]{0,1:T(8,128)(2,1)} %copy-done.1, bf16[4096,512]{0,1:T(8,128)(2,1)} %get-tuple-element.31, bf16[1,4096,512]{1,2,0:T(8,128)(2,1)} %copy.10, f32[4096]{0:T(1024)S(1)} %multiply_multiply_fusion, f32[4096]{0:T(1024)S(1)} %copy-done.8), kind=kLoop, calls=%fused_computation.52 | loop fusion | flops 14680064 | bytes 16809984 | tf_op jit(solution)/shard_map/broadcast_in_dim | solution.py:44
  462.4 6.4 %copy.11 = bf16[1,4096,512]{2,1,0:T(8,128)(2,1)} copy(bf16[1,4096,512]{1,2,0:T(8,128)(2,1)} %fusion.27) | data formatting | bytes 8388608
  468.8 39.0 %all-reduce.3.cloned.1.call-done = (bf16[1,64,1280]{2,1,0:T(8,128)(2,1)}, bf16[1,64,1280]{2,1,0:T(8,128)(2,1)}, bf16[1,64,1280]{2,1,0:T(8,128)(2,1)}, bf16[1,64,...) async-done(((bf16[1,64,1280]{2,1,0:T(8,128)(2,1)}, bf16[1,64,1280]{2,1,0:T(8,128)(2,1)}, bf16[1,64,1280]{2,1,0:T(8,128)(2,1)}, ...) | async-done | bytes 983056 | tf_op jit(solution)/shard_map/psum | solution.py:31
  507.8 1.7 pad_maximum_fusion.2
  509.5 2.0 pad_maximum_fusion
  (53 shorter events, 0.7 us)
Async XLA Ops:
  7.2 30.3 %all-gather.13.cloned.1.call-start = ((), (), s32[]{:S(2)}) async-start(), calls=%async_computation.12 | async-start | bytes 1474560 | tf_op jit(solution)/shard_map/all_gather | solution.py:28
  9.0 54.6 %all-gather.15.cloned.1.call-start = ((), (), s32[]{:S(2)}) async-start(), calls=%async_computation.13 | async-start | bytes 1474560 | tf_op jit(solution)/shard_map/all_gather | solution.py:28
  10.8 78.9 %all-gather.17.cloned.1.call-start = ((), (), s32[]{:S(2)}) async-start(), calls=%async_computation.14 | async-start | bytes 1474560 | tf_op jit(solution)/shard_map/all_gather | solution.py:28
  12.6 103.0 %all-gather.21.cloned.1.call-start = ((), (), s32[]{:S(2)}) async-start(), calls=%async_computation.16 | async-start | bytes 1474560 | tf_op jit(solution)/shard_map/all_gather | solution.py:28
  13.2 129.0 %all-gather.23.cloned.1.call-start = ((), (), s32[]{:S(2)}) async-start(), calls=%async_computation.17 | async-start | bytes 1474560 | tf_op jit(solution)/shard_map/all_gather | solution.py:28
  13.8 155.0 %all-gather.19.cloned.1.call-start = ((), (), s32[]{:S(2)}) async-start(), calls=%async_computation.15 | async-start | bytes 1474560 | tf_op jit(solution)/shard_map/all_gather | solution.py:28
  14.4 354.5 %reduce-scatter.17.cloned.1.call-start = ((), (), s32[]{:S(2)}) async-start(), calls=%async_computation.11 | async-start | bytes 1474560 | tf_op jit(solution)/shard_map/reduce_scatter | solution.py:31
  23.8 0.6 copy-start.3
  24.4 39.1 %copy-start.7 = (f32[4096]{0:T(1024)}, f32[4096]{0:T(1024)S(1)}, u32[]{:S(2)}) copy-start(f32[4096]{0:T(1024)S(1)} %fusion.59) | copy-start | bytes 49156
  100.9 0.6 copy-start.5
  197.5 18.6 %copy-start.12 = (bf16[1,512,1280]{2,1,0:T(8,128)(2,1)S(1)}, bf16[1,512,1280]{2,1,0:T(8,128)(2,1)}, u32[]{:S(2)}) copy-start(bf16[1,512,1280]{2,1,0:T(8,128)(2,1)} %all-gather.23.cloned.1.call-done) | copy-start | bytes 3932164
  216.1 15.4 %copy-start.13 = (bf16[1,512,1280]{2,1,0:T(8,128)(2,1)S(1)}, bf16[1,512,1280]{2,1,0:T(8,128)(2,1)}, u32[]{:S(2)}) copy-start(bf16[1,512,1280]{2,1,0:T(8,128)(2,1)} %all-gather.19.cloned.1.call-done) | copy-start | bytes 3932164
  216.1 152.8 %reduce-scatter.9.cloned.1.call-start = ((), (), s32[]{:S(2)}) async-start(), calls=%async_computation.7 | async-start | bytes 1474560 | tf_op jit(solution)/shard_map/reduce_scatter | solution.py:31
  216.2 15.4 %copy-start.2 = (bf16[4096,512]{0,1:T(8,128)(2,1)S(1)}, bf16[4096,512]{0,1:T(8,128)(2,1)}, u32[]{:S(2)}) copy-start(bf16[4096,512]{0,1:T(8,128)(2,1)} %get-tuple-element.23) | copy-start | bytes 12582916
  231.5 12.7 %copy-start.6 = (f32[4096]{0:T(1024)S(1)}, f32[4096]{0:T(1024)}, u32[]{:S(2)}) copy-start(f32[4096]{0:T(1024)} %copy-done.5) | copy-start | bytes 49156
  231.5 12.7 %copy-start.14 = (bf16[4096,1280]{1,0:T(8,128)(2,1)S(1)}, bf16[4096,1280]{1,0:T(8,128)(2,1)}, u32[]{:S(2)}) copy-start(bf16[4096,1280]{1,0:T(8,128)(2,1)} %get-tuple-element.24) | copy-start | bytes 31457284
  251.0 118.0 %reduce-scatter.15.cloned.1.call-start = ((), (), s32[]{:S(2)}) async-start(), calls=%async_computation.10 | async-start | bytes 1474560 | tf_op jit(solution)/shard_map/reduce_scatter | solution.py:31
  257.2 2.0 copy-start.1
  268.9 16.5 %copy-start.11 = (bf16[1,1280,512]{2,1,0:T(8,128)(2,1)S(1)}, bf16[1,1280,512]{2,1,0:T(8,128)(2,1)}, u32[]{:S(2)}) copy-start(bf16[1,1280,512]{2,1,0:T(8,128)(2,1)} %all-gather.17.cloned.1.call-done) | copy-start | bytes 3932164
  268.9 105.3 %reduce-scatter.13.cloned.1.call-start = ((), (), s32[]{:S(2)}) async-start(), calls=%async_computation.9 | async-start | bytes 1474560 | tf_op jit(solution)/shard_map/reduce_scatter | solution.py:31
  285.3 129.2 %reduce-scatter.7.cloned.1.call-start = ((), (), s32[]{:S(2)}) async-start(), calls=%async_computation.6 | async-start | bytes 1474560 | tf_op jit(solution)/shard_map/reduce_scatter | solution.py:31
  285.3 27.7 %copy-start.8 = (f32[4096]{0:T(1024)S(1)}, f32[4096]{0:T(1024)}, u32[]{:S(2)}) copy-start(f32[4096]{0:T(1024)} %copy-done.7) | copy-start | bytes 49156
  324.3 130.4 %reduce-scatter.11.cloned.1.call-start = ((), (), s32[]{:S(2)}) async-start(), calls=%async_computation.8 | async-start | bytes 1474560 | tf_op jit(solution)/shard_map/reduce_scatter | solution.py:31
  324.4 16.5 %copy-start.10 = (bf16[1,512,1280]{2,1,0:T(8,128)(2,1)S(1)}, bf16[1,512,1280]{2,1,0:T(8,128)(2,1)}, u32[]{:S(2)}) copy-start(bf16[1,512,1280]{2,1,0:T(8,128)(2,1)} %all-gather.15.cloned.1.call-done) | copy-start | bytes 3932164
  340.8 15.7 %copy-start.9 = (bf16[1,512,1280]{2,1,0:T(8,128)(2,1)S(1)}, bf16[1,512,1280]{2,1,0:T(8,128)(2,1)}, u32[]{:S(2)}) copy-start(bf16[1,512,1280]{2,1,0:T(8,128)(2,1)} %all-gather.13.cloned.1.call-done) | copy-start | bytes 3932164
  340.8 167.0 %all-reduce.3.cloned.1.call-start = ((), (), s32[]{:S(2)}) async-start(), calls=%async_computation.18 | async-start | bytes 1966080 | tf_op jit(solution)/shard_map/psum | solution.py:31
  340.8 15.6 %copy-start = (bf16[1,4096,512]{1,2,0:T(8,128)(2,1)S(1)}, bf16[1,4096,512]{1,2,0:T(8,128)(2,1)}, u32[]{:S(2)}) copy-start(bf16[1,4096,512]{1,2,0:T(8,128)(2,1)} %copy.10) | copy-start | bytes 12582916
  356.5 12.4 %copy-start.4 = (f32[4096]{0:T(1024)S(1)}, f32[4096]{0:T(1024)}, u32[]{:S(2)}) copy-start(f32[4096]{0:T(1024)} %copy-done.3) | copy-start | bytes 49156
Sparse Core Ops, SparseCore 0:
  10.4 26.9 all-gather.12
  39.3 24.1 all-gather.14
  65.4 24.1 all-gather.16
  91.4 24.1 all-gather.20
  118.0 24.1 all-gather.22
  144.5 24.1 all-gather.18
  216.2 37.0 reduce-scatter.16
  256.5 37.0 reduce-scatter.8
  296.9 37.0 reduce-scatter.14
  337.1 37.0 reduce-scatter.12
  377.4 37.0 reduce-scatter.6
  417.6 37.0 reduce-scatter.10
  457.6 50.1 all-reduce.2
where the time goes:
time: 528 us; the launch traced here: 519 us
  matrix products  256 us (48%)
  waiting for transfers between devices  199 us (38%)
  local copies, waits for them, and re-layouts  27.6 us (5%)
  other arithmetic  20.7 us (4%)
  between operations  14.5 us (3%)
    dot_general x6, matrix products, layer(): up = jnp.dot(a, w['w_up'], preferred_element_type=jnp.float32)  94.8 us
    reduce_scatter x6, waiting for transfers between devices, summed(): lax.psum_scatter(term, 's', scatter_dimension=0, tiled=True)  85.8 us
    dot_general x6, matrix products, layer(): gate = jnp.dot(a, w['w_gate'], preferred_element_type=jnp.float32)  83.6 us
    dot_general x5, matrix products, matmul(): jnp.dot(a, w, preferred_element_type=jnp.float32).astype(jnp.bfloat16)  77.4 us
    all_gather x6, waiting for transfers between devices, fetched(): lax.all_gather(w[number], 's', axis=0, tiled=True)  72.7 us
    psum x1, waiting for transfers between devices, summed(): lax.psum(lax.psum_scatter(term, 's', scatter_dimension=0, tiled=True), 'r')  39 us
    unnamed x33, local copies, waits for them, and re-layouts  22.4 us
  transfers between devices with their start and end apart: 13, of which 10 were waited for; matrix products, arithmetic and copies ran while one was open for 48% of the time, Pallas kernels for 0%

commit v1 on v0

v1 whole, which is shorter than its diff:
```python
import functools

import jax
import jax.numpy as jnp
from jax import lax
from jax.experimental import pallas as pl
from jax.experimental.pallas import tpu as pltpu
from jax.sharding import PartitionSpec as P

MESH = pl.DeviceIdType.MESH
F32, BF16 = jnp.float32, jnp.bfloat16
W = 256
S, R = 8, 4


def dot(a, b, dims):
    return lax.dot_general(a, b, (dims, ((), ())), preferred_element_type=F32)


NN, NT = ((1,), (0,)), ((1,), (1,))


def mean_square(wide):
    return jnp.mean(wide * wide, axis=-1, keepdims=True) + 1e-6


def kernel(
    tokens, d, ff, tile, small,
    x_ref, dy_ref, wg_ref, wu_ref, wd_ref,
    dx_ref, og_ref, ou_ref, od_ref, keep_a, keep_at,
    WG, WU, WD, A, AT, H, DH, DG, DU, ACC,
    C, R1, O1, B2, R2, O2, B3, R3, B4, OGU, OD,
    in_sem, own_sem, keep_sem, gs_sem, gr_sem, fs_sem, fr_sem,
    s1_sem, r1_sem, s2_sem, r2_sem, s3_sem, r3_sem, s4_sem, r4_sem, rd_sem, out_sem, dx_sem,
):
    z, s = lax.axis_index("r"), lax.axis_index("s")
    core, yy, xx = s % 2, (s // 2) % 2, s // 4
    xy = s // 2
    chunks = ff // W
    rows_d, rows_f = d // S, ff // S

    def at(px, py, pc):
        return 4 * px + 2 * py + pc

    def to(sem_s, sem_r, src, dst, r, dev):
        return pltpu.make_async_remote_copy(
            src_ref=src, dst_ref=dst, send_sem=sem_s, recv_sem=sem_r,
            device_id={"r": r, "s": dev}, device_id_type=MESH)

    sib = at(xx, yy, 1 - core)
    others = (at(1 - xx, yy, core), at(xx, 1 - yy, core), at(1 - xx, 1 - yy, core))

    mats = ((wg_ref, WG, rows_d), (wu_ref, WU, rows_d), (wd_ref, WD, rows_f))

    def block(m, l, dev):
        _, full, rows = mats[m]
        return full.at[l, pl.ds(pl.multiple_of(dev * rows, rows), rows)]

    def spread(m, l):
        return [to(gs_sem.at[l, m, i], gr_sem.at[l, m, i], mats[m][0].at[l], block(m, l, s), z, dev)
                for i, dev in enumerate(others + (sib,))]

    def onward(m, l):
        return [to(fs_sem.at[l, m, i], fr_sem.at[l, m, i], block(m, l, dev), block(m, l, dev), z, sib)
                for i, dev in enumerate(others)]

    def own(m, l):
        return pltpu.make_async_copy(mats[m][0].at[l], block(m, l, s), own_sem.at[l, m])

    def forward(l, ms):
        for m in ms:
            first, second = spread(m, l), onward(m, l)
            for i in range(3):
                first[i].wait_recv()
                second[i].start()

    def arrived(l, ms):
        for m in ms:
            own(m, l).wait()
            spread(m, l)[3].wait_recv()
            for copy in onward(m, l):
                copy.wait_recv()

    for l in range(2):
        for m in range(3):
            for copy in spread(m, l):
                copy.start()
    tiles, few = tokens // tile, tokens // small

    def x_in(i):
        r = pl.ds(i * small, small)
        return (pltpu.make_async_copy(x_ref.at[0, r], H.at[r], in_sem.at[0, i]),
                pltpu.make_async_copy(dy_ref.at[0, r], DH.at[r], in_sem.at[1, i]))

    for i in range(few):
        for copy in x_in(i):
            copy.start()
    for l in range(2):
        for m in range(3):
            own(m, l).start()

    def enter(i, _):
        r = pl.ds(pl.multiple_of(i * small, small), small)
        pltpu.make_async_copy(x_ref.at[0, r], H.at[r], in_sem.at[0, i]).wait()
        pltpu.make_async_copy(dy_ref.at[0, r], DH.at[r], in_sem.at[1, i]).wait()
        wide = H[r, :].astype(F32)
        a = (wide * lax.rsqrt(mean_square(wide))).astype(BF16)
        A[r, :] = a
        AT[:, r] = a.T
        return 0

    lax.fori_loop(0, few, enter, 0)
    keep = (pltpu.make_async_copy(A, keep_a, keep_sem.at[0]), pltpu.make_async_copy(AT, keep_at, keep_sem.at[1]))
    for copy in keep:
        copy.start()

    def columns(c):
        return pl.ds(pl.multiple_of(c * W, W), W)

    forward(0, (0, 1))
    arrived(0, (0, 1))

    def gated(i, _):
        c, t = i // tiles, i % tiles
        r, cs = pl.ds(pl.multiple_of(t * tile, tile), tile), columns(c)
        a = A[r, :]
        g, u = dot(a, WG[0, :, cs], NN), dot(a, WU[0, :, cs], NN)
        DG[r, cs] = (g * (1.0 / (1.0 + jnp.exp(-g))) * u).astype(BF16)
        return 0

    lax.fori_loop(0, 2 * tiles, gated, 0)
    forward(0, (2,))
    lax.fori_loop(2 * tiles, chunks * tiles, gated, 0)
    arrived(0, (2,))
    for copy in keep:
        copy.wait()

    def down(i, _):
        r = pl.ds(pl.multiple_of(i * small, small), small)
        h = H[r, :].astype(F32) + dot(DG[r, :], WD[0], NN).astype(BF16).astype(F32)
        H[r, :] = h.astype(BF16)
        wide = h.astype(BF16).astype(F32)
        a = (wide * lax.rsqrt(mean_square(wide))).astype(BF16)
        A[r, :] = a
        AT[:, r] = a.T
        return 0

    lax.fori_loop(0, few // 2, down, 0)
    forward(1, (0, 1, 2))
    lax.fori_loop(few // 2, few, down, 0)
    arrived(1, (0, 1, 2))

    def first_hop(k):
        slot = k % 2
        return to(s1_sem.at[0], r1_sem.at[slot], C.at[1 - core], R1.at[slot], z, sib)

    def second_hop(k):
        slot = k % 2
        places = ((1 - xx) * 2 + yy, xx * 2 + 1 - yy, (1 - xx) * 2 + 1 - yy)
        return [to(s2_sem.at[i], r2_sem.at[slot, i], B2.at[places[i]], R2.at[slot, i], z, others[i]) for i in range(3)]

    def third_hop(k):
        slot = k % 2
        return [to(s3_sem.at[i], r3_sem.at[slot, i], B3.at[(z + 1 + i) % R], R3.at[slot, i], (z + 1 + i) % R, s)
                for i in range(3)]

    def spread_gu(l, c):
        return [to(s4_sem.at[i], r4_sem.at[l, c, i], B4.at[pl.ds(0, 2)],
                   OGU.at[l, :, pl.ds(pl.multiple_of(z * 16, 16), 16), columns(c)], (z + 1 + i) % R, s)
                for i in range(3)]

    def place_d(p, zz):
        return (pl.ds(pl.multiple_of((p % chunks) * 32 + (zz // 2) * 16, 16), 16),
                pl.ds(pl.multiple_of((zz % 2) * W, W), W))

    def spread_d(l, c, zz):
        p = S * c + s
        rows, cols = place_d(p, z)
        return to(s4_sem.at[3 + zz], rd_sem.at[l, p % chunks, z], B4.at[2], OD.at[l, rows, cols], zz, p // chunks)

    def each_d(c, fn):
        for zz in range(R):
            @pl.when(jnp.logical_not(jnp.logical_and((S * c + s) // chunks == s, z == zz)))
            def _(zz=zz):
                fn(zz)

    def wait_fourth(l, c):
        for copy in spread_gu(l, c):
            copy.wait_send()
        each_d(c, lambda zz: spread_d(l, c, zz).wait_send())

    def stage_1(l, c, k):
        first_hop(k).wait()
        mine = C.at[core]
        got = R1.at[k % 2]
        for i in range(4):
            total = mine[i].astype(F32) + got[i].astype(F32)
            B2[i] = total.astype(BF16)

            @pl.when(i == xy)
            def _(total=total):
                O1[...] = total

        for copy in second_hop(k):
            copy.start()

    def stage_2(l, c, k):
        for copy in second_hop(k):
            copy.wait()
        slot = k % 2
        for i in range(R):
            total = O1[i]
            for j in range(3):
                total = total + R2[slot, j, i].astype(F32)
            B3[i] = total.astype(BF16)

            @pl.when(i == z)
            def _(total=total):
                O2[...] = total

        for copy in third_hop(k):
            copy.start()

    def stage_3(l, c, k):
        for copy in third_hop(k):
            copy.wait()

        @pl.when(k > 0)
        def _():
            before = k - 1
            wait_fourth(1 - before // chunks, before % chunks)

        slot = k % 2
        total = O2[...]
        for j in range(3):
            total = total + R3[slot, j].astype(F32)
        total = total.astype(BF16)
        B4[...] = total
        OGU[l, :, pl.ds(pl.multiple_of(z * 16, 16), 16), columns(c)] = total[0:2]
        p = S * c + s

        @pl.when(p // chunks == s)
        def _():
            rows, cols = place_d(p, z)
            OD[l, rows, cols] = total[2]

        for copy in spread_gu(l, c):
            copy.start()
        each_d(c, lambda zz: spread_d(l, c, zz).start())

    def at_step(t, when, l, c, k):
        for stage, step in zip((stage_1, stage_2, stage_3), when):
            @pl.when(t == step)
            def _(stage=stage):
                stage(l, c, k)

    def layer(li, _):
        l = 1 - li

        def chunk(c, _):
            k = li * chunks + c
            cs = columns(c)

            def part(t, _):
                r = pl.ds(pl.multiple_of(t * tile, tile), tile)
                a = A[r, :]
                g, u = dot(a, WG[l, :, cs], NN), dot(a, WU[l, :, cs], NN)
                dz = dot(DH[r, :], WD[l, cs, :], NT).astype(BF16).astype(F32)
                gate = 1.0 / (1.0 + jnp.exp(-g))
                act = g * gate
                hidden = (act * u).astype(BF16)
                du = (dz * act).astype(BF16)
                dg = (dz * u * (gate + act * (1.0 - gate))).astype(BF16)
                DG[r, cs] = dg
                DU[r, cs] = du
                at_t = AT[:, r]
                new = (dot(at_t, dg, NN), dot(at_t, du, NN))
                low = dot(hidden, DH[r, :], ((0,), (0,)))

                @pl.when(t == 0)
                def _():
                    ACC[0], ACC[1] = new
                    ACC[2, pl.ds(0, W)] = low[:, :W]
                    ACC[2, pl.ds(W, W)] = low[:, W:]

                @pl.when(t > 0)
                def _():
                    ACC[0] += new[0]
                    ACC[1] += new[1]
                    ACC[2, pl.ds(0, W)] += low[:, :W]
                    ACC[2, pl.ds(W, W)] += low[:, W:]

                @pl.when(c > 0)
                def _():
                    at_step(t, (0, tiles - 2, tiles - 1), l, c - 1, k - 1)

                return 0

            lax.fori_loop(0, tiles, part, 0)
            for dev in range(S):
                for q in range(R):
                    to_block = C.at[dev % 2, dev // 2, q]
                    gu = pl.ds(rows_d * dev + 16 * q, 16)
                    to_block[0] = ACC[0, gu].astype(BF16)
                    to_block[1] = ACC[1, gu].astype(BF16)
                    to_block[2] = ACC[2, pl.ds((q % 2) * W + 32 * dev + 16 * (q // 2), 16)].astype(BF16)
            first_hop(k).start()
            return 0

        lax.fori_loop(0, chunks, chunk, 0)

        @pl.when(li == 0)
        def _():
            pltpu.make_async_copy(keep_a, A, keep_sem.at[0]).start()
            pltpu.make_async_copy(keep_at, AT, keep_sem.at[1]).start()

        def below(i, _):
            r = pl.ds(pl.multiple_of(i * small, small), small)
            da = dot(DG[r, :], WG[l], NT).astype(BF16).astype(F32) + dot(DU[r, :], WU[l], NT).astype(BF16).astype(F32)
            da = da.astype(BF16).astype(F32)
            wide = H[r, :].astype(F32)
            scale = lax.rsqrt(mean_square(wide))
            along = jnp.mean(da * wide, axis=-1, keepdims=True)
            by_h = (scale * da - wide * (scale * scale * scale * along)).astype(BF16)
            dh = (by_h.astype(F32) + DH[r, :].astype(F32)).astype(BF16)
            DH[r, :] = dh

            @pl.when(li == 0)
            def _():
                pltpu.make_async_copy(x_ref.at[0, r], H.at[r], in_sem.at[0, i]).start()

            @pl.when(li == 1)
            def _():
                pltpu.make_async_copy(DH.at[r], dx_ref.at[0, r], dx_sem.at[i]).start()

            at_step(i, (0, few // 2 - 1, few // 2 + 1), l, chunks - 1, li * chunks + chunks - 1)
            return 0

        lax.fori_loop(0, few, below, 0)

        @pl.when(li == 0)
        def _():
            pltpu.make_async_copy(keep_a, A, keep_sem.at[0]).wait()
            pltpu.make_async_copy(keep_at, AT, keep_sem.at[1]).wait()
            for i in range(few):
                x_in(i)[0].wait()

        return 0

    lax.fori_loop(0, 2, layer, 0)

    wait_fourth(0, chunks - 1)
    for l in range(2):
        for c in range(chunks):
            for copy in spread_gu(l, c):
                copy.wait_recv()
        for pos in range(chunks):
            p = s * chunks + pos
            for zz in range(R):
                @pl.when(jnp.logical_not(jnp.logical_and(p % S == s, z == zz)))
                def _(l=l, pos=pos, zz=zz):
                    rows, cols = place_d(pos, zz)
                    to(s4_sem.at[0], rd_sem.at[l, pos, zz], B4.at[2], OD.at[l, rows, cols], z, s).wait_recv()
    last = (pltpu.make_async_copy(OGU.at[:, 0], og_ref, out_sem.at[0]),
            pltpu.make_async_copy(OGU.at[:, 1], ou_ref, out_sem.at[1]),
            pltpu.make_async_copy(OD, od_ref, out_sem.at[2]))
    for copy in last:
        copy.start()
    for l in range(2):
        for m in range(3):
            for copy in spread(m, l) + onward(m, l):
                copy.wait_send()
    for i in range(few):
        r = pl.ds(i * small, small)
        pltpu.make_async_copy(DH.at[r], dx_ref.at[0, r], dx_sem.at[i]).wait()
    for copy in last:
        copy.wait()


def whole(tokens, d, ff):
    tile, small = min(1024, tokens // 4), min(512, tokens // 8)
    few = tokens // small
    chunks = ff // W
    dma = pltpu.SemaphoreType.DMA
    layers = 2
    shape = jax.ShapeDtypeStruct
    rows_d, rows_f = d // S, ff // S
    any_space = pl.BlockSpec(memory_space=pl.ANY)
    flops = 2 * tokens * d * ff * 19
    return pl.pallas_call(
        functools.partial(kernel, tokens, d, ff, tile, small),
        out_shape=(
            shape((1, tokens, d), BF16), shape((layers, rows_d, ff), BF16), shape((layers, rows_d, ff), BF16),
            shape((layers, rows_f, d), BF16), shape((tokens, d), BF16), shape((d, tokens), BF16)),
        in_specs=[any_space] * 5,
        out_specs=(any_space,) * 6,
        scratch_shapes=[
            pltpu.VMEM((layers, d, ff), BF16), pltpu.VMEM((layers, d, ff), BF16), pltpu.VMEM((layers, ff, d), BF16),
            pltpu.VMEM((tokens, d), BF16), pltpu.VMEM((d, tokens), BF16),
            pltpu.VMEM((tokens, d), BF16), pltpu.VMEM((tokens, d), BF16),
            pltpu.VMEM((tokens, ff), BF16), pltpu.VMEM((tokens, ff), BF16),
            pltpu.VMEM((3, d, W), F32),
            pltpu.VMEM((2, 4, R, 3, 16, W), BF16), pltpu.VMEM((2, 4, R, 3, 16, W), BF16),
            pltpu.VMEM((R, 3, 16, W), F32), pltpu.VMEM((4, R, 3, 16, W), BF16),
            pltpu.VMEM((2, 3, R, 3, 16, W), BF16), pltpu.VMEM((3, 16, W), F32),
            pltpu.VMEM((R, 3, 16, W), BF16), pltpu.VMEM((2, 3, 3, 16, W), BF16),
            pltpu.VMEM((3, 16, W), BF16),
            pltpu.VMEM((layers, 2, rows_d, ff), BF16), pltpu.VMEM((layers, rows_f, d), BF16),
            dma((2, few)), dma((layers, 3)), dma((2,)),
            dma((layers, 3, 4)), dma((layers, 3, 4)), dma((layers, 3, 3)), dma((layers, 3, 3)),
            dma((1,)), dma((2,)), dma((3,)), dma((2, 3)), dma((3,)), dma((2, 3)),
            dma((7,)), dma((layers, chunks, 3)), dma((layers, chunks, R)), dma((3,)), dma((few,)),
        ],
        compiler_params=pltpu.CompilerParams(has_side_effects=True, vmem_limit_bytes=67_043_328),
        cost_estimate=pl.CostEstimate(flops=flops, bytes_accessed=4 * tokens * d * 2, transcendentals=0),
        name="stack",
    )


def solution(mesh):
    def step(x, dy, w_gate, w_up, w_down):
        _, tokens, d = x.shape
        ff = w_gate.shape[2]
        return whole(tokens, d, ff)(x, dy, w_gate, w_up, w_down)[:4]

    states, cut = P(("rep", "r", "s"), None, None), P(None, "s", None)
    return jax.shard_map(
        step,
        mesh=mesh,
        in_specs=(states, states) + (cut,) * 3,
        out_specs=(states,) + (P("rep", "s", None),) * 3,
        check_vma=False,
    )
```

time: 528 us -> 224 us (0.42); the launches traced: 519 us -> 224 us
  matrix products: 256 us -> 0 us
  Pallas kernels: 0 us -> 217 us
  waiting for transfers between devices: 199 us -> 0 us
  local copies, waits for them, and re-layouts: 27.6 us -> 6.74 us
  other arithmetic: 20.7 us -> 0 us
  between operations: 14.5 us -> 0.67 us
    dot_general x17 -> x0, matrix products: 256 us -> none  [the longest x6 94.8 us: layer(): up = jnp.dot(a, w['w_up'], preferred_element_type=jnp.float32)]
    pallas_call x0 -> x1, Pallas kernels: none -> 217 us  [step(): return whole(tokens, d, ff)(x, dy, w_gate, w_up, w_down)[:4]]
    reduce_scatter x6 -> x0, waiting for transfers between devices: 85.8 us -> none  [summed(): lax.psum_scatter(term, 's', scatter_dimension=0, tiled=True)]
    all_gather x6 -> x0, waiting for transfers between devices: 72.7 us -> none  [fetched(): lax.all_gather(w[number], 's', axis=0, tiled=True)]
    psum x1 -> x0, waiting for transfers between devices: 39 us -> none  [summed(): lax.psum(lax.psum_scatter(term, 's', scatter_dimension=0, tiled=True), 'r')]
    unnamed x33 -> x10, local copies, waits for them, and re-layouts: 22.4 us -> 6.74 us
    broadcast_in_dim x1 -> x0, other arithmetic: 7.62 us -> none  [step(): by_h[None]]
    add_any x1 -> x0, other arithmetic: 6.22 us -> none  [normed(): wide = h.astype(jnp.float32)]
  transfers between devices with their start and end apart: 13 -> 0, of which waited for: 10 -> 0; matrix products, arithmetic and copies ran while one was open for 48% -> 0% of each run, Pallas kernels for 0% -> 0%
where the time goes in v1:
time: 224 us
  Pallas kernels  217 us (97%)
  local copies, waits for them, and re-layouts  6.74 us (3%)
    pallas_call x1, Pallas kernels, step(): return whole(tokens, d, ff)(x, dy, w_gate, w_up, w_down)[:4]  217 us
    unnamed x10, local copies, waits for them, and re-layouts  6.74 us

profile of v1, /device:TPU:0, one launch (start us, length us, event | category | flops | bytes accessed | tf_op | source)
XLA Modules:
  0.0 224.3 jit_solution(17259910295240318737)
XLA Ops:
  0.6 216.9 %stack.1 = (bf16[1,4096,512]{2,1,0:T(8,128)(2,1)}, bf16[2,64,1280]{2,1,0:T(8,128)(2,1)}, bf16[2,64,1280]{2,1,0:T(8,128)(2,1)}, bf16[2,160,512]{2,1,0:T(8,128)(2,...) custom-call(bf16[1,4096,512]{2,1,0:T(8,128)(2,1)} %x_ref.1, bf16[1,4096,512]{2,1,0:T(8,128)(2,1)} %dy_ref.1, ...), custom_call_target="tpu_custom_call" | custom-call | flops 102005473280 | bytes 16777216 | tf_op jit(solution)/shard_map/stack/pallas_call | solution.py:424
  217.5 0.0 copy-start.2
  217.5 0.0 copy-start.1
  217.6 0.0 copy-start
  217.6 4.6 %copy.13 = bf16[1,4096,512]{2,1,0:T(8,128)(2,1)} copy(bf16[1,4096,512]{2,1,0:T(8,128)(2,1)} %get-tuple-element.16) | data formatting | bytes 8388608
  222.1 0.0 copy-done.2
  222.1 0.7 copy.14
  222.8 0.0 copy-done.1
  222.8 0.7 copy.15
  223.6 0.0 copy-done
  223.6 0.7 copy.16
Async XLA Ops:
  217.5 4.6 %copy-start.2 = (bf16[2,64,1280]{2,1,0:T(8,128)(2,1)S(1)}, bf16[2,64,1280]{2,1,0:T(8,128)(2,1)}, u32[]{:S(2)}) copy-start(bf16[2,64,1280]{2,1,0:T(8,128)(2,1)} %get-tuple-element.17) | copy-start | bytes 983044
  217.5 5.3 %copy-start.1 = (bf16[2,64,1280]{2,1,0:T(8,128)(2,1)S(1)}, bf16[2,64,1280]{2,1,0:T(8,128)(2,1)}, u32[]{:S(2)}) copy-start(bf16[2,64,1280]{2,1,0:T(8,128)(2,1)} %get-tuple-element.18) | copy-start | bytes 983044
  217.6 6.0 %copy-start = (bf16[2,160,512]{2,1,0:T(8,128)(2,1)S(1)}, bf16[2,160,512]{2,1,0:T(8,128)(2,1)}, u32[]{:S(2)}) copy-start(bf16[2,160,512]{2,1,0:T(8,128)(2,1)} %get-tuple-element.19) | copy-start | bytes 983044

commit v2 on v1

--- a/solution.py
+++ b/solution.py
@@ -28,7 +28,7 @@
     tokens, d, ff, tile, small,
     x_ref, dy_ref, wg_ref, wu_ref, wd_ref,
     dx_ref, og_ref, ou_ref, od_ref, keep_a, keep_at,
-    WG, WU, WD, A, AT, H, DH, DG, DU, ACC,
+    WG, WU, WD, A, AT, H, DH, DG, DU, Z,
     C, R1, O1, B2, R2, O2, B3, R3, B4, OGU, OD,
     in_sem, own_sem, keep_sem, gs_sem, gr_sem, fs_sem, fr_sem,
     s1_sem, r1_sem, s2_sem, r2_sem, s3_sem, r3_sem, s4_sem, r4_sem, rd_sem, out_sem, dx_sem,
@@ -52,40 +52,66 @@
 
     mats = ((wg_ref, WG, rows_d), (wu_ref, WU, rows_d), (wd_ref, WD, rows_f))
 
-    def block(m, l, dev):
+    def columns(c):
+        return pl.ds(pl.multiple_of(c * W, W), W)
+
+    def piece(l, m, c, dev):
         _, full, rows = mats[m]
-        return full.at[l, pl.ds(pl.multiple_of(dev * rows, rows), rows)]
-
-    def spread(m, l):
-        return [to(gs_sem.at[l, m, i], gr_sem.at[l, m, i], mats[m][0].at[l], block(m, l, s), z, dev)
-                for i, dev in enumerate(others + (sib,))]
-
-    def onward(m, l):
-        return [to(fs_sem.at[l, m, i], fr_sem.at[l, m, i], block(m, l, dev), block(m, l, dev), z, sib)
-                for i, dev in enumerate(others)]
-
-    def own(m, l):
-        return pltpu.make_async_copy(mats[m][0].at[l], block(m, l, s), own_sem.at[l, m])
-
-    def forward(l, ms):
+        r = pl.ds(pl.multiple_of(dev * rows, rows), rows)
+        return full.at[l, r] if m == 2 else full.at[l, r, columns(c)]
+
+    def mine(l, m, c):
+        return mats[m][0].at[l] if m == 2 else mats[m][0].at[l, :, columns(c)]
+
+    def spread(l, m, c, i):
+        return to(gs_sem.at[l, m, c, i], gr_sem.at[l, m, c, i], mine(l, m, c), piece(l, m, c, s), z, (others + (sib,))[i])
+
+    def onward(l, m, c, i):
+        block = piece(l, m, c, others[i])
+        return to(fs_sem.at[l, m, c, i], fr_sem.at[l, m, c, i], block, block, z, sib)
+
+    def own(l, m):
+        rows = mats[m][2]
+        return pltpu.make_async_copy(
+            mats[m][0].at[l], mats[m][1].at[l, pl.ds(pl.multiple_of(s * rows, rows), rows)], own_sem.at[l, m])
+
+    def send(l, ms, c):
         for m in ms:
-            first, second = spread(m, l), onward(m, l)
+            for i in range(4):
+                spread(l, m, c, i).start()
+
+    def forward(l, ms, c):
+        for m in ms:
             for i in range(3):
-                first[i].wait_recv()
-                second[i].start()
-
-    def arrived(l, ms):
+                spread(l, m, c, i).wait_recv()
+                onward(l, m, c, i).start()
+
+    def arrived(l, ms, c):
         for m in ms:
-            own(m, l).wait()
-            spread(m, l)[3].wait_recv()
-            for copy in onward(m, l):
-                copy.wait_recv()
-
-    for l in range(2):
-        for m in range(3):
-            for copy in spread(m, l):
-                copy.start()
+            spread(l, m, c, 3).wait_recv()
+            for i in range(3):
+                onward(l, m, c, i).wait_recv()
+
+    def sent(l, ms, c):
+        for m in ms:
+            for i in range(4):
+                spread(l, m, c, i).wait_send()
+            for i in range(3):
+                onward(l, m, c, i).wait_send()
+
+    GU, DOWN = (0, 1), (2,)
+    barrier = pltpu.get_barrier_semaphore()
+    here = z * S + s
+
+    def greet(i, _):
+        there = (here + i) % (R * S)
+        pl.semaphore_signal(barrier, inc=1, device_id={"r": there // S, "s": there % S}, device_id_type=MESH)
+        return 0
+
+    lax.fori_loop(1, R * S, greet, 0)
     tiles, few = tokens // tile, tokens // small
+    fine = small // 2
+    down_parts = tokens // fine
 
     def x_in(i):
         r = pl.ds(i * small, small)
@@ -97,12 +123,11 @@
             copy.start()
     for l in range(2):
         for m in range(3):
-            own(m, l).start()
+            own(l, m).start()
 
     def enter(i, _):
         r = pl.ds(pl.multiple_of(i * small, small), small)
         pltpu.make_async_copy(x_ref.at[0, r], H.at[r], in_sem.at[0, i]).wait()
-        pltpu.make_async_copy(dy_ref.at[0, r], DH.at[r], in_sem.at[1, i]).wait()
         wide = H[r, :].astype(F32)
         a = (wide * lax.rsqrt(mean_square(wide))).astype(BF16)
         A[r, :] = a
@@ -110,45 +135,63 @@
         return 0
 
     lax.fori_loop(0, few, enter, 0)
+    pl.semaphore_wait(barrier, R * S - 1)
+    for c in range(chunks):
+        send(0, GU, c)
+    send(0, DOWN, 0)
     keep = (pltpu.make_async_copy(A, keep_a, keep_sem.at[0]), pltpu.make_async_copy(AT, keep_at, keep_sem.at[1]))
     for copy in keep:
         copy.start()
 
-    def columns(c):
-        return pl.ds(pl.multiple_of(c * W, W), W)
-
-    forward(0, (0, 1))
-    arrived(0, (0, 1))
-
-    def gated(i, _):
-        c, t = i // tiles, i % tiles
-        r, cs = pl.ds(pl.multiple_of(t * tile, tile), tile), columns(c)
-        a = A[r, :]
-        g, u = dot(a, WG[0, :, cs], NN), dot(a, WU[0, :, cs], NN)
-        DG[r, cs] = (g * (1.0 / (1.0 + jnp.exp(-g))) * u).astype(BF16)
+    forward(0, GU, 0)
+    send(1, DOWN, 0)
+    for c in range(chunks):
+        send(1, GU, c)
+    for l in range(2):
+        for m in range(3):
+            own(l, m).wait()
+
+    def gated(c, _):
+        cs = columns(c)
+        arrived(0, GU, c)
+        for t in range(tiles):
+            if t == tiles // 2:
+                @pl.when(c < chunks - 1)
+                def _():
+                    forward(0, GU, c + 1)
+            r = pl.ds(t * tile, tile)
+            a = A[r, :]
+            g, u = dot(a, WG[0, :, cs], NN), dot(a, WU[0, :, cs], NN)
+            DG[r, cs] = (g * (1.0 / (1.0 + jnp.exp(-g))) * u).astype(BF16)
         return 0
 
-    lax.fori_loop(0, 2 * tiles, gated, 0)
-    forward(0, (2,))
-    lax.fori_loop(2 * tiles, chunks * tiles, gated, 0)
-    arrived(0, (2,))
+    lax.fori_loop(0, chunks, gated, 0)
+    forward(0, DOWN, 0)
+    for i in range(few):
+        x_in(i)[1].wait()
+    arrived(0, DOWN, 0)
     for copy in keep:
         copy.wait()
 
     def down(i, _):
-        r = pl.ds(pl.multiple_of(i * small, small), small)
-        h = H[r, :].astype(F32) + dot(DG[r, :], WD[0], NN).astype(BF16).astype(F32)
-        H[r, :] = h.astype(BF16)
-        wide = h.astype(BF16).astype(F32)
-        a = (wide * lax.rsqrt(mean_square(wide))).astype(BF16)
-        A[r, :] = a
-        AT[:, r] = a.T
+        for q in range(down_parts // 2):
+            r = pl.ds(pl.multiple_of((i * (down_parts // 2) + q) * fine, fine), fine)
+            h = (H[r, :].astype(F32) + dot(DG[r, :], WD[0], NN).astype(BF16).astype(F32)).astype(BF16)
+            H[r, :] = h
+            wide = h.astype(F32)
+            a = (wide * lax.rsqrt(mean_square(wide))).astype(BF16)
+            A[r, :] = a
+            AT[:, r] = a.T
+
+        @pl.when(i == 0)
+        def _():
+            forward(1, DOWN, 0)
+
         return 0
 
-    lax.fori_loop(0, few // 2, down, 0)
-    forward(1, (0, 1, 2))
-    lax.fori_loop(few // 2, few, down, 0)
-    arrived(1, (0, 1, 2))
+    lax.fori_loop(0, 2, down, 0)
+    forward(1, GU, 0)
+    arrived(1, DOWN, 0)
 
     def first_hop(k):
         slot = k % 2
@@ -191,10 +234,10 @@
 
     def stage_1(l, c, k):
         first_hop(k).wait()
-        mine = C.at[core]
+        kept = C.at[core]
         got = R1.at[k % 2]
         for i in range(4):
-            total = mine[i].astype(F32) + got[i].astype(F32)
+            total = kept[i].astype(F32) + got[i].astype(F32)
             B2[i] = total.astype(BF16)
 
             @pl.when(i == xy)
@@ -248,12 +291,6 @@
             copy.start()
         each_d(c, lambda zz: spread_d(l, c, zz).start())
 
-    def at_step(t, when, l, c, k):
-        for stage, step in zip((stage_1, stage_2, stage_3), when):
-            @pl.when(t == step)
-            def _(stage=stage):
-                stage(l, c, k)
-
     def layer(li, _):
         l = 1 - li
 
@@ -261,49 +298,41 @@
             k = li * chunks + c
             cs = columns(c)
 
-            def part(t, _):
-                r = pl.ds(pl.multiple_of(t * tile, tile), tile)
+            @pl.when(li == 0)
+            def _():
+                arrived(1, GU, c)
+
+            for t in range(tiles):
+                r = pl.ds(t * tile, tile)
                 a = A[r, :]
                 g, u = dot(a, WG[l, :, cs], NN), dot(a, WU[l, :, cs], NN)
                 dz = dot(DH[r, :], WD[l, cs, :], NT).astype(BF16).astype(F32)
                 gate = 1.0 / (1.0 + jnp.exp(-g))
                 act = g * gate
-                hidden = (act * u).astype(BF16)
-                du = (dz * act).astype(BF16)
-                dg = (dz * u * (gate + act * (1.0 - gate))).astype(BF16)
-                DG[r, cs] = dg
-                DU[r, cs] = du
-                at_t = AT[:, r]
-                new = (dot(at_t, dg, NN), dot(at_t, du, NN))
-                low = dot(hidden, DH[r, :], ((0,), (0,)))
-
-                @pl.when(t == 0)
-                def _():
-                    ACC[0], ACC[1] = new
-                    ACC[2, pl.ds(0, W)] = low[:, :W]
-                    ACC[2, pl.ds(W, W)] = low[:, W:]
-
-                @pl.when(t > 0)
-                def _():
-                    ACC[0] += new[0]
-                    ACC[1] += new[1]
-                    ACC[2, pl.ds(0, W)] += low[:, :W]
-                    ACC[2, pl.ds(W, W)] += low[:, W:]
-
-                @pl.when(c > 0)
-                def _():
-                    at_step(t, (0, tiles - 2, tiles - 1), l, c - 1, k - 1)
-
-                return 0
-
-            lax.fori_loop(0, tiles, part, 0)
+                Z[r, :] = (act * u).astype(BF16)
+                DU[r, cs] = (dz * act).astype(BF16)
+                DG[r, cs] = (dz * u * (gate + act * (1.0 - gate))).astype(BF16)
+
+            @pl.when(jnp.logical_and(li == 0, c < chunks - 1))
+            def _():
+                forward(1, GU, c + 1)
+
+            for back, stage in ((3, stage_3), (2, stage_2), (1, stage_1)):
+                @pl.when(c >= back)
+                def _(back=back, stage=stage):
+                    stage(l, c - back, k - back)
+
+            by_gate = dot(AT[...], DG[:, cs], NN).astype(BF16)
+            by_up = dot(AT[...], DU[:, cs], NN).astype(BF16)
+            by_down = dot(Z[...], DH[...], ((0,), (0,))).astype(BF16)
             for dev in range(S):
                 for q in range(R):
                     to_block = C.at[dev % 2, dev // 2, q]
-                    gu = pl.ds(rows_d * dev + 16 * q, 16)
-                    to_block[0] = ACC[0, gu].astype(BF16)
-                    to_block[1] = ACC[1, gu].astype(BF16)
-                    to_block[2] = ACC[2, pl.ds((q % 2) * W + 32 * dev + 16 * (q // 2), 16)].astype(BF16)
+                    top = rows_d * dev + 16 * q
+                    to_block[0] = by_gate[top:top + 16]
+                    to_block[1] = by_up[top:top + 16]
+                    top = 32 * dev + 16 * (q // 2)
+                    to_block[2] = by_down[top:top + 16, (q % 2) * W:(q % 2) * W + W]
             first_hop(k).start()
             return 0
 
@@ -316,14 +345,15 @@
 
         def below(i, _):
             r = pl.ds(pl.multiple_of(i * small, small), small)
-            da = dot(DG[r, :], WG[l], NT).astype(BF16).astype(F32) + dot(DU[r, :], WU[l], NT).astype(BF16).astype(F32)
-            da = da.astype(BF16).astype(F32)
-            wide = H[r, :].astype(F32)
-            scale = lax.rsqrt(mean_square(wide))
-            along = jnp.mean(da * wide, axis=-1, keepdims=True)
-            by_h = (scale * da - wide * (scale * scale * scale * along)).astype(BF16)
-            dh = (by_h.astype(F32) + DH[r, :].astype(F32)).astype(BF16)
-            DH[r, :] = dh
+            for q in range(2):
+                r2 = pl.ds(pl.multiple_of(i * small + q * fine, fine), fine)
+                da = (dot(DG[r2, :], WG[l], NT).astype(BF16).astype(F32)
+                      + dot(DU[r2, :], WU[l], NT).astype(BF16).astype(F32)).astype(BF16).astype(F32)
+                wide = H[r2, :].astype(F32)
+                scale = lax.rsqrt(mean_square(wide))
+                along = jnp.mean(da * wide, axis=-1, keepdims=True)
+                by_h = (scale * da - wide * (scale * scale * scale * along)).astype(BF16)
+                DH[r2, :] = (by_h.astype(F32) + DH[r2, :].astype(F32)).astype(BF16)
 
             @pl.when(li == 0)
             def _():
@@ -333,7 +363,12 @@
             def _():
                 pltpu.make_async_copy(DH.at[r], dx_ref.at[0, r], dx_sem.at[i]).start()
 
-            at_step(i, (0, few // 2 - 1, few // 2 + 1), l, chunks - 1, li * chunks + chunks - 1)
+            k = li * chunks + chunks - 1
+            for step, stage, back in ((0, stage_3, 2), (0, stage_2, 1), (0, stage_1, 0), (3, stage_3, 1), (3, stage_2, 0), (5, stage_3, 0)):
+                @pl.when(i == step * few // 8)
+                def _(stage=stage, back=back):
+                    stage(l, chunks - 1 - back, k - back)
+
             return 0
 
         lax.fori_loop(0, few, below, 0)
@@ -367,9 +402,13 @@
     for copy in last:
         copy.start()
     for l in range(2):
-        for m in range(3):
-            for copy in spread(m, l) + onward(m, l):
-                copy.wait_send()
+        sent(l, DOWN, 0)
+
+        def all_sent(c, _, l=l):
+            sent(l, GU, c)
+            return 0
+
+        lax.fori_loop(0, chunks, all_sent, 0)
     for i in range(few):
         r = pl.ds(i * small, small)
         pltpu.make_async_copy(DH.at[r], dx_ref.at[0, r], dx_sem.at[i]).wait()
@@ -399,7 +438,7 @@
             pltpu.VMEM((tokens, d), BF16), pltpu.VMEM((d, tokens), BF16),
             pltpu.VMEM((tokens, d), BF16), pltpu.VMEM((tokens, d), BF16),
             pltpu.VMEM((tokens, ff), BF16), pltpu.VMEM((tokens, ff), BF16),
-            pltpu.VMEM((3, d, W), F32),
+            pltpu.VMEM((tokens, W), BF16),
             pltpu.VMEM((2, 4, R, 3, 16, W), BF16), pltpu.VMEM((2, 4, R, 3, 16, W), BF16),
             pltpu.VMEM((R, 3, 16, W), F32), pltpu.VMEM((4, R, 3, 16, W), BF16),
             pltpu.VMEM((2, 3, R, 3, 16, W), BF16), pltpu.VMEM((3, 16, W), F32),
@@ -407,11 +446,11 @@
             pltpu.VMEM((3, 16, W), BF16),
             pltpu.VMEM((layers, 2, rows_d, ff), BF16), pltpu.VMEM((layers, rows_f, d), BF16),
             dma((2, few)), dma((layers, 3)), dma((2,)),
-            dma((layers, 3, 4)), dma((layers, 3, 4)), dma((layers, 3, 3)), dma((layers, 3, 3)),
+            dma((layers, 3, chunks, 4)), dma((layers, 3, chunks, 4)), dma((layers, 3, chunks, 3)), dma((layers, 3, chunks, 3)),
             dma((1,)), dma((2,)), dma((3,)), dma((2, 3)), dma((3,)), dma((2, 3)),
             dma((7,)), dma((layers, chunks, 3)), dma((layers, chunks, R)), dma((3,)), dma((few,)),
         ],
-        compiler_params=pltpu.CompilerParams(has_side_effects=True, vmem_limit_bytes=67_043_328),
+        compiler_params=pltpu.CompilerParams(has_side_effects=True, collective_id=0, vmem_limit_bytes=67_043_328),
         cost_estimate=pl.CostEstimate(flops=flops, bytes_accessed=4 * tokens * d * 2, transcendentals=0),
         name="stack",
     )

time: 224 us -> 170 us (0.76)
  Pallas kernels: 217 us -> 162 us
    pallas_call x1, Pallas kernels: 217 us -> 162 us  [step(): return whole(tokens, d, ff)(x, dy, w_gate, w_up, w_down)[:4]]
where the time goes in v2:
time: 170 us
  Pallas kernels  162 us (95%)
  local copies, waits for them, and re-layouts  6.74 us (4%)
    pallas_call x1, Pallas kernels, step(): return whole(tokens, d, ff)(x, dy, w_gate, w_up, w_down)[:4]  162 us
    unnamed x10, local copies, waits for them, and re-layouts  6.74 us

profile of v2, /device:TPU:0, one launch (start us, length us, event | category | flops | bytes accessed | tf_op | source)
XLA Modules:
  0.0 169.9 jit_solution(16137543907999662025)
XLA Ops:
  0.6 162.5 %stack.1 = (bf16[1,4096,512]{2,1,0:T(8,128)(2,1)}, bf16[2,64,1280]{2,1,0:T(8,128)(2,1)}, bf16[2,64,1280]{2,1,0:T(8,128)(2,1)}, bf16[2,160,512]{2,1,0:T(8,128)(2,...) custom-call(bf16[1,4096,512]{2,1,0:T(8,128)(2,1)} %x_ref.1, bf16[1,4096,512]{2,1,0:T(8,128)(2,1)} %dy_ref.1, ...), custom_call_target="tpu_custom_call" | custom-call | flops 102005473280 | bytes 16777216 | tf_op jit(solution)/shard_map/stack/pallas_call | solution.py:463
  163.1 0.0 copy-start.2
  163.1 0.0 copy-start.1
  163.1 0.0 copy-start
  163.1 4.6 %copy.13 = bf16[1,4096,512]{2,1,0:T(8,128)(2,1)} copy(bf16[1,4096,512]{2,1,0:T(8,128)(2,1)} %get-tuple-element.16) | data formatting | bytes 8388608
  167.7 0.0 copy-done.2
  167.7 0.7 copy.14
  168.4 0.0 copy-done.1
  168.4 0.7 copy.15
  169.1 0.0 copy-done
  169.1 0.7 copy.16
Async XLA Ops:
  163.1 4.6 %copy-start.2 = (bf16[2,64,1280]{2,1,0:T(8,128)(2,1)S(1)}, bf16[2,64,1280]{2,1,0:T(8,128)(2,1)}, u32[]{:S(2)}) copy-start(bf16[2,64,1280]{2,1,0:T(8,128)(2,1)} %get-tuple-element.17) | copy-start | bytes 983044
  163.1 5.3 %copy-start.1 = (bf16[2,64,1280]{2,1,0:T(8,128)(2,1)S(1)}, bf16[2,64,1280]{2,1,0:T(8,128)(2,1)}, u32[]{:S(2)}) copy-start(bf16[2,64,1280]{2,1,0:T(8,128)(2,1)} %get-tuple-element.18) | copy-start | bytes 983044
  163.1 6.0 %copy-start = (bf16[2,160,512]{2,1,0:T(8,128)(2,1)S(1)}, bf16[2,160,512]{2,1,0:T(8,128)(2,1)}, u32[]{:S(2)}) copy-start(bf16[2,160,512]{2,1,0:T(8,128)(2,1)} %get-tuple-element.19) | copy-start | bytes 983044

commit v3 on v2

--- a/solution.py
+++ b/solution.py
@@ -27,11 +27,11 @@
 def kernel(
     tokens, d, ff, tile, small,
     x_ref, dy_ref, wg_ref, wu_ref, wd_ref,
-    dx_ref, og_ref, ou_ref, od_ref, keep_a, keep_at,
-    WG, WU, WD, A, AT, H, DH, DG, DU, Z,
+    dx_ref, og_ref, ou_ref, od_ref, keep_a, keep_at, keep_f, keep_z,
+    WG, WU, WD, A, AT, H, DH, DG, DU, Z, F,
     C, R1, O1, B2, R2, O2, B3, R3, B4, OGU, OD,
     in_sem, own_sem, keep_sem, gs_sem, gr_sem, fs_sem, fr_sem,
-    s1_sem, r1_sem, s2_sem, r2_sem, s3_sem, r3_sem, s4_sem, r4_sem, rd_sem, out_sem, dx_sem,
+    s1_sem, r1_sem, s2_sem, r2_sem, s3_sem, r3_sem, s4_sem, r4_sem, rd_sem, out_sem, dx_sem, f_sem, z_sem,
 ):
     z, s = lax.axis_index("r"), lax.axis_index("s")
     core, yy, xx = s % 2, (s // 2) % 2, s // 4
@@ -151,21 +151,47 @@
         for m in range(3):
             own(l, m).wait()
 
-    def gated(c, _):
-        cs = columns(c)
-        arrived(0, GU, c)
-        for t in range(tiles):
-            if t == tiles // 2:
-                @pl.when(c < chunks - 1)
-                def _():
-                    forward(0, GU, c + 1)
-            r = pl.ds(t * tile, tile)
-            a = A[r, :]
-            g, u = dot(a, WG[0, :, cs], NN), dot(a, WU[0, :, cs], NN)
-            DG[r, cs] = (g * (1.0 / (1.0 + jnp.exp(-g))) * u).astype(BF16)
+    def factors_out(c, t):
+        r = pl.ds(pl.multiple_of(t * tile, tile), tile)
+        return pltpu.make_async_copy(F.at[:, r], keep_f.at[c, :, r], f_sem.at[t])
+
+    def factors_in(c, t):
+        r = pl.ds(t * tile, tile)
+        return pltpu.make_async_copy(keep_f.at[c, :, r], F.at[:, r], f_sem.at[t])
+
+    def hidden_in(c):
+        return pltpu.make_async_copy(keep_z.at[:, columns(c)], Z, z_sem.at[0])
+
+    def gated(i, _):
+        c, t = i // tiles, i % tiles
+        r, cs = pl.ds(pl.multiple_of(t * tile, tile), tile), columns(c)
+
+        @pl.when(t == 0)
+        def _():
+            arrived(0, GU, c)
+
+        @pl.when(c > 0)
+        def _():
+            factors_out(c - 1, t).wait()
+
+        a = A[r, :]
+        g, u = dot(a, WG[0, :, cs], NN), dot(a, WU[0, :, cs], NN)
+        gate = 1.0 / (1.0 + jnp.exp(-g))
+        act = g * gate
+        DG[r, cs] = (act * u).astype(BF16)
+        F[0, r] = act
+        F[1, r] = u * (gate + act * (1.0 - gate))
+        factors_out(c, t).start()
+
+        @pl.when(jnp.logical_and(t == 1, c < chunks - 1))
+        def _():
+            forward(0, GU, c + 1)
+
         return 0
 
-    lax.fori_loop(0, chunks, gated, 0)
+    lax.fori_loop(0, chunks * tiles, gated, 0)
+    all_hidden = pltpu.make_async_copy(DG, keep_z, z_sem.at[0])
+    all_hidden.start()
     forward(0, DOWN, 0)
     for i in range(few):
         x_in(i)[1].wait()
@@ -192,6 +218,9 @@
     lax.fori_loop(0, 2, down, 0)
     forward(1, GU, 0)
     arrived(1, DOWN, 0)
+    all_hidden.wait()
+    for t in range(tiles):
+        factors_out(chunks - 1, t).wait()
 
     def first_hop(k):
         slot = k % 2
@@ -302,16 +331,34 @@
             def _():
                 arrived(1, GU, c)
 
-            for t in range(tiles):
-                r = pl.ds(t * tile, tile)
-                a = A[r, :]
-                g, u = dot(a, WG[l, :, cs], NN), dot(a, WU[l, :, cs], NN)
-                dz = dot(DH[r, :], WD[l, cs, :], NT).astype(BF16).astype(F32)
-                gate = 1.0 / (1.0 + jnp.exp(-g))
-                act = g * gate
-                Z[r, :] = (act * u).astype(BF16)
-                DU[r, cs] = (dz * act).astype(BF16)
-                DG[r, cs] = (dz * u * (gate + act * (1.0 - gate))).astype(BF16)
+            @pl.when(li == 0)
+            def _():
+                for t in range(tiles):
+                    r = pl.ds(t * tile, tile)
+                    a = A[r, :]
+                    g, u = dot(a, WG[1, :, cs], NN), dot(a, WU[1, :, cs], NN)
+                    dz = dot(DH[r, :], WD[1, cs, :], NT).astype(BF16).astype(F32)
+                    gate = 1.0 / (1.0 + jnp.exp(-g))
+                    act = g * gate
+                    Z[r, :] = (act * u).astype(BF16)
+                    DU[r, cs] = (dz * act).astype(BF16)
+                    DG[r, cs] = (dz * (u * (gate + act * (1.0 - gate)))).astype(BF16)
+
+            @pl.when(li == 1)
+            def _():
+                for t in range(tiles):
+                    factors_in(c, t).wait()
+                for t in range(tiles):
+                    r = pl.ds(t * tile, tile)
+                    dz = dot(DH[r, :], WD[0, cs, :], NT).astype(BF16).astype(F32)
+                    DU[r, cs] = (dz * F[0, r]).astype(BF16)
+                    DG[r, cs] = (dz * F[1, r]).astype(BF16)
+                hidden_in(c).wait()
+
+                @pl.when(c < chunks - 1)
+                def _():
+                    for t in range(tiles):
+                        factors_in(c + 1, t).start()
 
             @pl.when(jnp.logical_and(li == 0, c < chunks - 1))
             def _():
@@ -334,6 +381,11 @@
                     top = 32 * dev + 16 * (q // 2)
                     to_block[2] = by_down[top:top + 16, (q % 2) * W:(q % 2) * W + W]
             first_hop(k).start()
+
+            @pl.when(jnp.logical_and(li == 1, c < chunks - 1))
+            def _():
+                hidden_in(c + 1).start()
+
             return 0
 
         lax.fori_loop(0, chunks, chunk, 0)
@@ -342,6 +394,9 @@
         def _():
             pltpu.make_async_copy(keep_a, A, keep_sem.at[0]).start()
             pltpu.make_async_copy(keep_at, AT, keep_sem.at[1]).start()
+            hidden_in(0).start()
+            for t in range(tiles):
+                factors_in(0, t).start()
 
         def below(i, _):
             r = pl.ds(pl.multiple_of(i * small, small), small)
@@ -425,20 +480,21 @@
     shape = jax.ShapeDtypeStruct
     rows_d, rows_f = d // S, ff // S
     any_space = pl.BlockSpec(memory_space=pl.ANY)
-    flops = 2 * tokens * d * ff * 19
+    flops = 2 * tokens * d * ff * 17
     return pl.pallas_call(
         functools.partial(kernel, tokens, d, ff, tile, small),
         out_shape=(
             shape((1, tokens, d), BF16), shape((layers, rows_d, ff), BF16), shape((layers, rows_d, ff), BF16),
-            shape((layers, rows_f, d), BF16), shape((tokens, d), BF16), shape((d, tokens), BF16)),
+            shape((layers, rows_f, d), BF16), shape((tokens, d), BF16), shape((d, tokens), BF16),
+            shape((chunks, 2, tokens, W), F32), shape((tokens, ff), BF16)),
         in_specs=[any_space] * 5,
-        out_specs=(any_space,) * 6,
+        out_specs=(any_space,) * 8,
         scratch_shapes=[
             pltpu.VMEM((layers, d, ff), BF16), pltpu.VMEM((layers, d, ff), BF16), pltpu.VMEM((layers, ff, d), BF16),
             pltpu.VMEM((tokens, d), BF16), pltpu.VMEM((d, tokens), BF16),
             pltpu.VMEM((tokens, d), BF16), pltpu.VMEM((tokens, d), BF16),
             pltpu.VMEM((tokens, ff), BF16), pltpu.VMEM((tokens, ff), BF16),
-            pltpu.VMEM((tokens, W), BF16),
+            pltpu.VMEM((tokens, W), BF16), pltpu.VMEM((2, tokens, W), F32),
             pltpu.VMEM((2, 4, R, 3, 16, W), BF16), pltpu.VMEM((2, 4, R, 3, 16, W), BF16),
             pltpu.VMEM((R, 3, 16, W), F32), pltpu.VMEM((4, R, 3, 16, W), BF16),
             pltpu.VMEM((2, 3, R, 3, 16, W), BF16), pltpu.VMEM((3, 16, W), F32),
@@ -448,7 +504,7 @@
             dma((2, few)), dma((layers, 3)), dma((2,)),
             dma((layers, 3, chunks, 4)), dma((layers, 3, chunks, 4)), dma((layers, 3, chunks, 3)), dma((layers, 3, chunks, 3)),
             dma((1,)), dma((2,)), dma((3,)), dma((2, 3)), dma((3,)), dma((2, 3)),
-            dma((7,)), dma((layers, chunks, 3)), dma((layers, chunks, R)), dma((3,)), dma((few,)),
+            dma((7,)), dma((layers, chunks, 3)), dma((layers, chunks, R)), dma((3,)), dma((few,)), dma((tokens // tile,)), dma((1,)),
         ],
         compiler_params=pltpu.CompilerParams(has_side_effects=True, collective_id=0, vmem_limit_bytes=67_043_328),
         cost_estimate=pl.CostEstimate(flops=flops, bytes_accessed=4 * tokens * d * 2, transcendentals=0),

time: 170 us -> 163 us (0.959)
  Pallas kernels: 162 us -> 155 us
    pallas_call x1, Pallas kernels: 162 us -> 155 us  [step(): return whole(tokens, d, ff)(x, dy, w_gate, w_up, w_down)[:4]]
where the time goes in v3:
time: 163 us
  Pallas kernels  155 us (95%)
  local copies, waits for them, and re-layouts  6.74 us (4%)
    pallas_call x1, Pallas kernels, step(): return whole(tokens, d, ff)(x, dy, w_gate, w_up, w_down)[:4]  155 us
    unnamed x10, local copies, waits for them, and re-layouts  6.74 us

profile of v3, /device:TPU:0, one launch (start us, length us, event | category | flops | bytes accessed | tf_op | source)
XLA Modules:
  0.0 162.7 jit_solution(16436106402573089572)
XLA Ops:
  0.6 155.3 %stack.1 = (bf16[1,4096,512]{2,1,0:T(8,128)(2,1)}, bf16[2,64,1280]{2,1,0:T(8,128)(2,1)}, bf16[2,64,1280]{2,1,0:T(8,128)(2,1)}, bf16[2,160,512]{2,1,0:T(8,128)(2,...) custom-call(bf16[1,4096,512]{2,1,0:T(8,128)(2,1)} %x_ref.1, ...), custom_call_target="tpu_custom_call" | custom-call | flops 91268055040 | bytes 16777216 | tf_op jit(solution)/shard_map/stack/pallas_call | solution.py:519
  155.9 0.0 copy-start.2
  155.9 0.0 copy-start.1
  155.9 0.0 copy-start
  155.9 4.6 %copy.13 = bf16[1,4096,512]{2,1,0:T(8,128)(2,1)} copy(bf16[1,4096,512]{2,1,0:T(8,128)(2,1)} %get-tuple-element.16) | data formatting | bytes 8388608
  160.5 0.0 copy-done.2
  160.5 0.7 copy.14
  161.2 0.0 copy-done.1
  161.2 0.7 copy.15
  161.9 0.0 copy-done
  162.0 0.7 copy.16
Async XLA Ops:
  155.9 4.6 %copy-start.2 = (bf16[2,64,1280]{2,1,0:T(8,128)(2,1)S(1)}, bf16[2,64,1280]{2,1,0:T(8,128)(2,1)}, u32[]{:S(2)}) copy-start(bf16[2,64,1280]{2,1,0:T(8,128)(2,1)} %get-tuple-element.17) | copy-start | bytes 983044
  155.9 5.3 %copy-start.1 = (bf16[2,64,1280]{2,1,0:T(8,128)(2,1)S(1)}, bf16[2,64,1280]{2,1,0:T(8,128)(2,1)}, u32[]{:S(2)}) copy-start(bf16[2,64,1280]{2,1,0:T(8,128)(2,1)} %get-tuple-element.18) | copy-start | bytes 983044
  155.9 6.0 %copy-start = (bf16[2,160,512]{2,1,0:T(8,128)(2,1)S(1)}, bf16[2,160,512]{2,1,0:T(8,128)(2,1)}, u32[]{:S(2)}) copy-start(bf16[2,160,512]{2,1,0:T(8,128)(2,1)} %get-tuple-element.19) | copy-start | bytes 983044

commit v4 on v3

--- a/solution.py
+++ b/solution.py
@@ -183,7 +183,7 @@
         F[1, r] = u * (gate + act * (1.0 - gate))
         factors_out(c, t).start()
 
-        @pl.when(jnp.logical_and(t == 1, c < chunks - 1))
+        @pl.when(jnp.logical_and(t == 2, c < chunks - 1))
         def _():
             forward(0, GU, c + 1)
 
@@ -263,16 +263,9 @@
 
     def stage_1(l, c, k):
         first_hop(k).wait()
-        kept = C.at[core]
-        got = R1.at[k % 2]
-        for i in range(4):
-            total = kept[i].astype(F32) + got[i].astype(F32)
-            B2[i] = total.astype(BF16)
-
-            @pl.when(i == xy)
-            def _(total=total):
-                O1[...] = total
-
+        slot = k % 2
+        B2[...] = (C[core].astype(F32) + R1[slot].astype(F32)).astype(BF16)
+        O1[...] = C[core, xy].astype(F32) + R1[slot, xy].astype(F32)
         for copy in second_hop(k):
             copy.start()
 
@@ -280,16 +273,8 @@
         for copy in second_hop(k):
             copy.wait()
         slot = k % 2
-        for i in range(R):
-            total = O1[i]
-            for j in range(3):
-                total = total + R2[slot, j, i].astype(F32)
-            B3[i] = total.astype(BF16)
-
-            @pl.when(i == z)
-            def _(total=total):
-                O2[...] = total
-
+        B3[...] = (O1[...] + R2[slot, 0].astype(F32) + R2[slot, 1].astype(F32) + R2[slot, 2].astype(F32)).astype(BF16)
+        O2[...] = O1[z] + R2[slot, 0, z].astype(F32) + R2[slot, 1, z].astype(F32) + R2[slot, 2, z].astype(F32)
         for copy in third_hop(k):
             copy.start()
 
@@ -512,11 +497,43 @@
     )
 
 
+def hand_on(*refs):
+    n = len(refs) // 4
+    ins, outs, held, (sems,) = refs[:4], refs[4:8], refs[8:12], refs[12:]
+    parts = [(0, slice(512 * i, 512 * (i + 1))) for i in range(ins[0].shape[1] // 512)]
+    jobs = [(0, part) for part in parts] + [(i, (slice(None),)) for i in range(1, n + 3) if i < 4]
+    copies = []
+    for q, (i, (*lead, rows)) in enumerate(jobs):
+        at = (*lead, pl.ds(rows.start, 512)) if rows.start is not None else (pl.ds(0, ins[i].shape[0]),)
+        copies.append((pltpu.make_async_copy(ins[i].at[at], held[i].at[at], sems.at[0, q]),
+                       pltpu.make_async_copy(held[i].at[at], outs[i].at[at], sems.at[1, q])))
+    for into, _ in copies:
+        into.start()
+    for into, out in copies:
+        into.wait()
+        out.start()
+    for _, out in copies:
+        out.wait()
+
+
+def handed_on(*arrays):
+    any_space = pl.BlockSpec(memory_space=pl.ANY)
+    jobs = arrays[0].shape[1] // 512 + 3
+    return pl.pallas_call(
+        hand_on,
+        out_shape=tuple(jax.ShapeDtypeStruct(a.shape, a.dtype) for a in arrays),
+        in_specs=[any_space] * 4,
+        out_specs=(any_space,) * 4,
+        scratch_shapes=[pltpu.VMEM(a.shape, a.dtype) for a in arrays] + [pltpu.SemaphoreType.DMA((2, jobs))],
+        name="hand_on",
+    )(*arrays)
+
+
 def solution(mesh):
     def step(x, dy, w_gate, w_up, w_down):
         _, tokens, d = x.shape
         ff = w_gate.shape[2]
-        return whole(tokens, d, ff)(x, dy, w_gate, w_up, w_down)[:4]
+        return handed_on(*whole(tokens, d, ff)(x, dy, w_gate, w_up, w_down)[:4])
 
     states, cut = P(("rep", "r", "s"), None, None), P(None, "s", None)
     return jax.shard_map(

time: 163 us -> 160 us (0.982)
  local copies, waits for them, and re-layouts: 6.74 us -> 0 us
  Pallas kernels: 155 us -> 159 us
    unnamed x10 -> x0, local copies, waits for them, and re-layouts: 6.74 us -> none
    pallas_call x1 -> x2, Pallas kernels: 155 us -> 159 us  [the longest x1 154 us: step(): return handed_on(*whole(tokens, d, ff)(x, dy, w_gate, w_up, w_down)[:4])]
where the time goes in v4:
time: 160 us
  Pallas kernels  159 us (99%)
    pallas_call x1, Pallas kernels, step(): return handed_on(*whole(tokens, d, ff)(x, dy, w_gate, w_up, w_down)[:4])  154 us
    pallas_call x1, Pallas kernels, handed_on(): pl.pallas_call(hand_on, out_shape=tuple((jax.ShapeDtypeStruct(a.shape, a....  4.58 us

profile of v4, /device:TPU:0, one launch (start us, length us, event | category | flops | bytes accessed | tf_op | source)
XLA Modules:
  0.0 159.7 jit_solution(4409697092974396704)
XLA Ops:
  0.6 154.3 %stack.1 = (bf16[1,4096,512]{2,1,0:T(8,128)(2,1)}, bf16[2,64,1280]{2,1,0:T(8,128)(2,1)}, bf16[2,64,1280]{2,1,0:T(8,128)(2,1)}, bf16[2,160,512]{2,1,0:T(8,128)(2,...) custom-call(bf16[1,4096,512]{2,1,0:T(8,128)(2,1)} %x_ref.1, ...), custom_call_target="tpu_custom_call" | custom-call | flops 91268055040 | bytes 16777216 | tf_op jit(solution)/shard_map/stack/pallas_call | solution.py:536
  154.9 4.6 %hand_on.1 = (bf16[1,4096,512]{2,1,0:T(8,128)(2,1)}, bf16[2,64,1280]{2,1,0:T(8,128)(2,1)}, bf16[2,64,1280]{2,1,0:T(8,128)(2,1)}, bf16[2,160,512]{2,1,0:T(8,128)(2,1)}) custom-call(bf16[1,4096,512]{2,1,0:T(8,128)(2,1)} %get-tuple-element.8.refs_0_, bf16[2,64,1280]{2,1,0:T(8,128)(2,1)} %get-tuple-element.9.refs_1_, ...), custom_call_target="tpu_custom_call" | custom-call | tf_op jit(solution)/shard_map/hand_on/pallas_call | solution.py:522

commit v5 on v4

--- a/solution.py
+++ b/solution.py
@@ -318,8 +318,8 @@
 
             @pl.when(li == 0)
             def _():
-                for t in range(tiles):
-                    r = pl.ds(t * tile, tile)
+                for t in range(tiles // 2):
+                    r = pl.ds(t * 2 * tile, 2 * tile)
                     a = A[r, :]
                     g, u = dot(a, WG[1, :, cs], NN), dot(a, WU[1, :, cs], NN)
                     dz = dot(DH[r, :], WD[1, cs, :], NT).astype(BF16).astype(F32)
@@ -333,8 +333,8 @@
             def _():
                 for t in range(tiles):
                     factors_in(c, t).wait()
-                for t in range(tiles):
-                    r = pl.ds(t * tile, tile)
+                for t in range(tiles // 2):
+                    r = pl.ds(t * 2 * tile, 2 * tile)
                     dz = dot(DH[r, :], WD[0, cs, :], NT).astype(BF16).astype(F32)
                     DU[r, cs] = (dz * F[0, r]).astype(BF16)
                     DG[r, cs] = (dz * F[1, r]).astype(BF16)

time: 160 us -> 162 us (1.012)
  Pallas kernels: 159 us -> 161 us
    pallas_call x1, Pallas kernels: 154 us -> 156 us  [step(): return handed_on(*whole(tokens, d, ff)(x, dy, w_gate, w_up, w_down)[:4])]
where the time goes in v5:
time: 162 us
  Pallas kernels  161 us (99%)
    pallas_call x1, Pallas kernels, step(): return handed_on(*whole(tokens, d, ff)(x, dy, w_gate, w_up, w_down)[:4])  156 us
    pallas_call x1, Pallas kernels, handed_on(): pl.pallas_call(hand_on, out_shape=tuple((jax.ShapeDtypeStruct(a.shape, a....  4.58 us

profile of v5, /device:TPU:0, one launch (start us, length us, event | category | flops | bytes accessed | tf_op | source)
XLA Modules:
  0.0 161.9 jit_solution(13687498132885818889)
XLA Ops:
  0.6 156.5 %stack.1 = (bf16[1,4096,512]{2,1,0:T(8,128)(2,1)}, bf16[2,64,1280]{2,1,0:T(8,128)(2,1)}, bf16[2,64,1280]{2,1,0:T(8,128)(2,1)}, bf16[2,160,512]{2,1,0:T(8,128)(2,...) custom-call(bf16[1,4096,512]{2,1,0:T(8,128)(2,1)} %x_ref.1, ...), custom_call_target="tpu_custom_call" | custom-call | flops 91268055040 | bytes 16777216 | tf_op jit(solution)/shard_map/stack/pallas_call | solution.py:536
  157.1 4.6 %hand_on.1 = (bf16[1,4096,512]{2,1,0:T(8,128)(2,1)}, bf16[2,64,1280]{2,1,0:T(8,128)(2,1)}, bf16[2,64,1280]{2,1,0:T(8,128)(2,1)}, bf16[2,160,512]{2,1,0:T(8,128)(2,1)}) custom-call(bf16[1,4096,512]{2,1,0:T(8,128)(2,1)} %get-tuple-element.8.refs_0_, bf16[2,64,1280]{2,1,0:T(8,128)(2,1)} %get-tuple-element.9.refs_1_, ...), custom_call_target="tpu_custom_call" | custom-call | tf_op jit(solution)/shard_map/hand_on/pallas_call | solution.py:522
